TPU v7x, 32 devices: a whole 2x2x4 slice. The times are simulated.
32 devices in a mesh: dp: 8 (over z, x), seq: 4 (over y, core).
Axes of the slice: x: 2, y: 2, z: 4, core: 2. Of those that a mesh axis runs over, the one named last changes fastest.
Arguments:
- tokens: bfloat16 [16, 2048, 768], P('dp', 'seq'), may hold values from -6 to 6
- segment_ids: int32 [16, 2048], P('dp'), may hold values from 0 to 3, never falling along the last dimension, each value on 1 to 1024 neighbouring positions
- w_query: float32 [768, 768], P('dp'), may hold values from -0.3125 to 0.3125
- w_key: float32 [768, 768], P('dp'), may hold values from -0.3125 to 0.3125
- w_value: float32 [768, 768], P('dp'), may hold values from -0.21875 to 0.21875
- w_output: float32 [768, 768], P('dp'), may hold values from -0.875 to 0.875
- b_query: float32 [768], P('dp'), may hold values from -3 to 3
- b_value: float32 [768], P('dp'), may hold values from -3 to 3
- b_output: float32 [768], P('dp'), may hold values from -3 to 3
- first_gain: float32 [768], P('dp'), may hold values from 0.5 to 1.5
- first_shift: float32 [768], P('dp'), may hold values from -3 to 3
- w_inner: float32 [768, 3072], P('dp'), may hold values from -0.21875 to 0.21875
- b_inner: float32 [3072], P('dp'), may hold values from -3 to 3
- w_outer: float32 [3072, 768], P('dp'), may hold values from -0.109375 to 0.109375
- b_outer: float32 [768], P('dp'), may hold values from -3 to 3
- second_gain: float32 [768], P('dp'), may hold values from 0.5 to 1.5
- second_shift: float32 [768], P('dp'), may hold values from -3 to 3
- cotangent: bfloat16 [16, 2048, 768], P('dp', 'seq'), may hold values from -6 to 6
Outputs:
- mixed: bfloat16 [16, 2048, 768], P('dp', 'seq')
- grad_tokens: float32 [16, 2048, 768], P('dp', 'seq')
- grad_w_query: float32 [768, 768], P('dp')
- grad_w_key: float32 [768, 768], P('dp')
- grad_w_value: float32 [768, 768], P('dp')
- grad_w_output: float32 [768, 768], P('dp')
- grad_b_query: float32 [768], P('dp')
- grad_b_value: float32 [768], P('dp')
- grad_b_output: float32 [768], P('dp')
- grad_first_gain: float32 [768], P('dp')
- grad_first_shift: float32 [768], P('dp')
- grad_w_inner: float32 [768, 3072], P('dp')
- grad_b_inner: float32 [3072], P('dp')
- grad_w_outer: float32 [3072, 768], P('dp')
- grad_b_outer: float32 [768], P('dp')
- grad_second_gain: float32 [768], P('dp')
- grad_second_shift: float32 [768], P('dp')
Inputs may be any that keep to these rules, and one draw needn't show every extreme that they name: `segment_ids`: within each sequence the segment numbers never fall, and each of the 4 numbers covers 1 to 1024 positions.
All inputs are finite; a program needn't handle non-finite values.
Results may differ from a plain program's by a relative error of at most 0.017.
The roundings to bfloat16 on the way count: a program that leaves them out, or rounds other values in their place, can miss the bound.
Values may be sent and summed in bfloat16 or wider, within the bound.
A program may use at most 192 MiB of HBM per device.

v0:
```python
import jax
import jax.numpy as jnp
from jax import lax
from jax.sharding import PartitionSpec as P

HD = 64


EPS = 1e-12
MASKED = -1000000000.0
ROOT_HALF = 0.7071067811865476
INV_ROOT_TAU = 0.3989422804014327


def lowered(piece):
    return piece.astype(jnp.bfloat16)


def widen(piece):
    return piece.astype(jnp.float32)


def matmul(left, right):
    return jnp.dot(left, right, preferred_element_type=jnp.float32)


def matmul_tn(left, right):
    return lax.dot_general(
        left, right, (((0,), (0,)), ((), ())), preferred_element_type=jnp.float32
    )


def matmul_nt(left, right):
    return lax.dot_general(
        left, right, (((1,), (1,)), ((), ())), preferred_element_type=jnp.float32
    )


def normalize(hidden, norm_gain, norm_shift):
    centred = hidden - jnp.mean(hidden, axis=-1, keepdims=True)
    reciprocal = lax.rsqrt(jnp.mean(centred * centred, axis=-1, keepdims=True) + EPS)
    normed = centred * reciprocal
    return (normed * norm_gain + norm_shift, normed, reciprocal)


def normalize_back(upstream, normed, reciprocal, norm_gain):
    scaled = upstream * norm_gain
    result = reciprocal * (
        scaled
        - jnp.mean(scaled, axis=-1, keepdims=True)
        - normed * jnp.mean(scaled * normed, axis=-1, keepdims=True)
    )
    return (result, jnp.sum(upstream * normed, axis=0), jnp.sum(upstream, axis=0))


def gelu_value(values_in):
    return 0.5 * values_in * (1.0 + lax.erf(values_in * ROOT_HALF))


def gelu_slope(values_in):
    return (
        0.5 * (1.0 + lax.erf(values_in * ROOT_HALF))
        + values_in * jnp.exp(-0.5 * values_in * values_in) * INV_ROOT_TAU
    )


def split_heads(matrix):
    return matrix.reshape(matrix.shape[0], matrix.shape[1] // HD, HD)


def scores_of(query_heads, key_heads, row_segments, column_segments):
    products = jnp.einsum(
        "qhd,khd->hqk", query_heads, key_heads, preferred_element_type=jnp.float32
    ) * HD ** (-0.5)
    same_doc = row_segments[:, None] == column_segments[None, :]
    return jnp.where(same_doc[None], products, MASKED)


def attend(block):
    queries, key_rows, value_rows, segments = block
    length = queries.shape[0]
    block_rows = min(512, length)
    key_heads = split_heads(key_rows)
    value_heads = split_heads(value_rows)

    def one_block(index):
        start = index * block_rows
        query_block = lax.dynamic_slice_in_dim(queries, start, block_rows, 0)
        segment_block = lax.dynamic_slice_in_dim(segments, start, block_rows, 0)
        scores = scores_of(split_heads(query_block), key_heads, segment_block, segments)
        largest = jnp.max(scores, axis=-1, keepdims=True)
        exponent = jnp.exp(scores - largest)
        row_total = jnp.sum(exponent, axis=-1, keepdims=True)
        weights = (exponent / row_total).astype(jnp.bfloat16)
        context = jnp.einsum(
            "hqk,khd->qhd", weights, value_heads, preferred_element_type=jnp.float32
        )
        return (context.reshape(block_rows, -1).astype(jnp.bfloat16), largest + jnp.log(row_total))

    context_blocks, logsum = lax.map(one_block, jnp.arange(length // block_rows, dtype=jnp.int32))
    return (context_blocks.reshape(length, -1), logsum)


def attend_back(block):
    queries, key_rows, value_rows, segments, logsum, upstream = block
    length = queries.shape[0]
    block_rows = min(512, length)
    key_heads = split_heads(key_rows)
    value_heads = split_heads(value_rows)

    def one_block(carry, index):
        key_total, value_total = carry
        start = index * block_rows
        query_heads = split_heads(lax.dynamic_slice_in_dim(queries, start, block_rows, 0))
        upstream_heads = split_heads(lax.dynamic_slice_in_dim(upstream, start, block_rows, 0))
        segment_block = lax.dynamic_slice_in_dim(segments, start, block_rows, 0)
        weights = jnp.exp(
            scores_of(query_heads, key_heads, segment_block, segments) - logsum[index]
        )
        grad_weights = jnp.einsum(
            "qhd,khd->hqk", upstream_heads, value_heads, preferred_element_type=jnp.float32
        )
        value_total = value_total + jnp.einsum(
            "hqk,qhd->khd",
            weights.astype(jnp.bfloat16),
            upstream_heads,
            preferred_element_type=jnp.float32,
        )
        grad_scores = (
            weights * (grad_weights - jnp.sum(weights * grad_weights, axis=-1, keepdims=True))
        ).astype(jnp.bfloat16)
        grad_queries = jnp.einsum(
            "hqk,khd->qhd", grad_scores, key_heads, preferred_element_type=jnp.float32
        ) * HD ** (-0.5)
        key_total = key_total + jnp.einsum(
            "hqk,qhd->khd", grad_scores, query_heads, preferred_element_type=jnp.float32
        ) * HD ** (-0.5)
        return ((key_total, value_total), grad_queries.reshape(block_rows, -1).astype(jnp.bfloat16))

    empty = jnp.zeros(key_heads.shape, jnp.float32)
    (key_total, value_total), grad_query_blocks = lax.scan(
        one_block, (empty, empty), jnp.arange(length // block_rows, dtype=jnp.int32)
    )
    return (
        grad_query_blocks.reshape(length, -1),
        key_total.reshape(length, -1).astype(jnp.bfloat16),
        value_total.reshape(length, -1).astype(jnp.bfloat16),
    )


def reduce_every(terms):
    owned = (
        lax.psum_scatter(terms[0], "dp", scatter_dimension=0, tiled=True),
        lax.psum_scatter(terms[1], "dp", scatter_dimension=0, tiled=True),
        lax.psum_scatter(terms[2], "dp", scatter_dimension=0, tiled=True),
        lax.psum_scatter(terms[3], "dp", scatter_dimension=0, tiled=True),
        lax.psum_scatter(terms[4], "dp", scatter_dimension=0, tiled=True),
        lax.psum_scatter(terms[5], "dp", scatter_dimension=0, tiled=True),
        lax.psum_scatter(terms[6], "dp", scatter_dimension=0, tiled=True),
        lax.psum_scatter(terms[7], "dp", scatter_dimension=0, tiled=True),
        lax.psum_scatter(terms[8], "dp", scatter_dimension=0, tiled=True),
        lax.psum_scatter(terms[9], "dp", scatter_dimension=0, tiled=True),
        lax.psum_scatter(terms[10], "dp", scatter_dimension=0, tiled=True),
        lax.psum_scatter(terms[11], "dp", scatter_dimension=0, tiled=True),
        lax.psum_scatter(terms[12], "dp", scatter_dimension=0, tiled=True),
        lax.psum_scatter(terms[13], "dp", scatter_dimension=0, tiled=True),
        lax.psum_scatter(terms[14], "dp", scatter_dimension=0, tiled=True),
    )
    return (
        lax.psum(owned[0].astype(jnp.bfloat16), "seq").astype(jnp.float32),
        lax.psum(owned[1].astype(jnp.bfloat16), "seq").astype(jnp.float32),
        lax.psum(owned[2].astype(jnp.bfloat16), "seq").astype(jnp.float32),
        lax.psum(owned[3].astype(jnp.bfloat16), "seq").astype(jnp.float32),
        lax.psum(owned[4].astype(jnp.bfloat16), "seq").astype(jnp.float32),
        lax.psum(owned[5].astype(jnp.bfloat16), "seq").astype(jnp.float32),
        lax.psum(owned[6].astype(jnp.bfloat16), "seq").astype(jnp.float32),
        lax.psum(owned[7].astype(jnp.bfloat16), "seq").astype(jnp.float32),
        lax.psum(owned[8].astype(jnp.bfloat16), "seq").astype(jnp.float32),
        lax.psum(owned[9].astype(jnp.bfloat16), "seq").astype(jnp.float32),
        lax.psum(owned[10].astype(jnp.bfloat16), "seq").astype(jnp.float32),
        lax.psum(owned[11].astype(jnp.bfloat16), "seq").astype(jnp.float32),
        lax.psum(owned[12].astype(jnp.bfloat16), "seq").astype(jnp.float32),
        lax.psum(owned[13].astype(jnp.bfloat16), "seq").astype(jnp.float32),
        lax.psum(owned[14].astype(jnp.bfloat16), "seq").astype(jnp.float32),
    )


def body(
    tokens,
    segment_ids,
    w_query,
    w_key,
    w_value,
    w_output,
    b_query,
    b_value,
    b_output,
    first_gain,
    first_shift,
    w_inner,
    b_inner,
    w_outer,
    b_outer,
    second_gain,
    second_shift,
    cotangent,
):
    gathered = (
        lax.all_gather(lowered(w_query), "dp", axis=0, tiled=True),
        lax.all_gather(lowered(w_key), "dp", axis=0, tiled=True),
        lax.all_gather(lowered(w_value), "dp", axis=0, tiled=True),
        lax.all_gather(lowered(w_output), "dp", axis=0, tiled=True),
        lax.all_gather(lowered(b_query), "dp", axis=0, tiled=True),
        lax.all_gather(lowered(b_value), "dp", axis=0, tiled=True),
        lax.all_gather(lowered(b_output), "dp", axis=0, tiled=True),
        lax.all_gather(lowered(first_gain), "dp", axis=0, tiled=True),
        lax.all_gather(lowered(first_shift), "dp", axis=0, tiled=True),
        lax.all_gather(lowered(w_inner), "dp", axis=0, tiled=True),
        lax.all_gather(lowered(b_inner), "dp", axis=0, tiled=True),
        lax.all_gather(lowered(w_outer), "dp", axis=0, tiled=True),
        lax.all_gather(lowered(b_outer), "dp", axis=0, tiled=True),
        lax.all_gather(lowered(second_gain), "dp", axis=0, tiled=True),
        lax.all_gather(lowered(second_shift), "dp", axis=0, tiled=True),
    )
    (
        full_query,
        full_key,
        full_value,
        full_output,
        bias_query,
        bias_value,
        bias_output,
        gain_first,
        shift_first,
        full_inner,
        bias_inner,
        full_outer,
        bias_outer,
        gain_second,
        shift_second,
    ) = gathered
    sequences, local_len, model_width = tokens.shape
    row_count = sequences * local_len
    inputs = tokens.reshape(row_count, model_width)
    queries = (matmul(inputs, full_query) + widen(bias_query)).astype(jnp.bfloat16)
    key_rows = matmul(inputs, full_key).astype(jnp.bfloat16)
    value_rows = (matmul(inputs, full_value) + widen(bias_value)).astype(jnp.bfloat16)
    head_queries, head_keys, head_values = (
        lax.all_to_all(
            queries.reshape(sequences, local_len, model_width),
            "seq",
            split_axis=2,
            concat_axis=1,
            tiled=True,
        ),
        lax.all_to_all(
            key_rows.reshape(sequences, local_len, model_width),
            "seq",
            split_axis=2,
            concat_axis=1,
            tiled=True,
        ),
        lax.all_to_all(
            value_rows.reshape(sequences, local_len, model_width),
            "seq",
            split_axis=2,
            concat_axis=1,
            tiled=True,
        ),
    )
    context_heads, logsum = lax.map(attend, (head_queries, head_keys, head_values, segment_ids))
    context = lax.all_to_all(context_heads, "seq", split_axis=1, concat_axis=2, tiled=True).reshape(
        row_count, model_width
    )
    attended = matmul(context, full_output) + widen(bias_output)
    first, first_normed, first_recip = normalize(
        widen(inputs) + attended, widen(gain_first), widen(shift_first)
    )
    first_low = first.astype(jnp.bfloat16)
    inner = matmul(first_low, full_inner) + widen(bias_inner)
    active = gelu_value(inner).astype(jnp.bfloat16)
    outer = matmul(active, full_outer) + widen(bias_outer)
    mixed, second_normed, second_recip = normalize(
        first + outer, widen(gain_second), widen(shift_second)
    )
    (
        back_query,
        back_key,
        back_value,
        back_output,
        back_gain_first,
        back_inner,
        back_outer,
        back_gain_second,
    ) = (
        lax.all_gather(lowered(w_query), "dp", axis=0, tiled=True),
        lax.all_gather(lowered(w_key), "dp", axis=0, tiled=True),
        lax.all_gather(lowered(w_value), "dp", axis=0, tiled=True),
        lax.all_gather(lowered(w_output), "dp", axis=0, tiled=True),
        lax.all_gather(lowered(first_gain), "dp", axis=0, tiled=True),
        lax.all_gather(lowered(w_inner), "dp", axis=0, tiled=True),
        lax.all_gather(lowered(w_outer), "dp", axis=0, tiled=True),
        lax.all_gather(lowered(second_gain), "dp", axis=0, tiled=True),
    )
    upstream = widen(cotangent.reshape(row_count, model_width))
    pre_second, grad_second_gain, grad_second_shift = normalize_back(
        upstream, second_normed, second_recip, widen(back_gain_second)
    )
    grad_outer = pre_second.astype(jnp.bfloat16)
    grad_b_outer = jnp.sum(widen(grad_outer), axis=0)
    grad_w_outer = matmul_tn(active, grad_outer)
    grad_inner = (matmul_nt(grad_outer, back_outer) * gelu_slope(inner)).astype(jnp.bfloat16)
    grad_b_inner = jnp.sum(widen(grad_inner), axis=0)
    grad_w_inner = matmul_tn(first_low, grad_inner)
    grad_first = pre_second + matmul_nt(grad_inner, back_inner)
    dense_terms = (
        grad_w_inner,
        grad_b_inner,
        grad_w_outer,
        grad_b_outer,
        grad_second_gain,
        grad_second_shift,
    )
    pre_first, grad_first_gain, grad_first_shift = normalize_back(
        grad_first, first_normed, first_recip, widen(back_gain_first)
    )
    grad_attended = pre_first.astype(jnp.bfloat16)
    grad_b_output = jnp.sum(widen(grad_attended), axis=0)
    grad_w_output = matmul_tn(context, grad_attended)
    grad_context = (
        matmul_nt(grad_attended, back_output)
        .astype(jnp.bfloat16)
        .reshape(sequences, local_len, model_width)
    )
    grad_context_heads = lax.all_to_all(
        grad_context, "seq", split_axis=2, concat_axis=1, tiled=True
    )
    head_grads = lax.map(
        attend_back, (head_queries, head_keys, head_values, segment_ids, logsum, grad_context_heads)
    )
    grad_queries, grad_keys, grad_values = (
        lax.all_to_all(head_grads[0], "seq", split_axis=1, concat_axis=2, tiled=True),
        lax.all_to_all(head_grads[1], "seq", split_axis=1, concat_axis=2, tiled=True),
        lax.all_to_all(head_grads[2], "seq", split_axis=1, concat_axis=2, tiled=True),
    )
    grad_queries = grad_queries.reshape(row_count, model_width)
    grad_keys = grad_keys.reshape(row_count, model_width)
    grad_values = grad_values.reshape(row_count, model_width)
    grad_b_query = jnp.sum(widen(grad_queries), axis=0)
    grad_b_value = jnp.sum(widen(grad_values), axis=0)
    grad_w_query = matmul_tn(inputs, grad_queries)
    grad_w_key = matmul_tn(inputs, grad_keys)
    grad_w_value = matmul_tn(inputs, grad_values)
    grad_tokens = (
        pre_first
        + matmul_nt(grad_queries, back_query)
        + matmul_nt(grad_keys, back_key)
        + matmul_nt(grad_values, back_value)
    )
    attention_terms = (
        grad_w_query,
        grad_w_key,
        grad_w_value,
        grad_w_output,
        grad_b_query,
        grad_b_value,
        grad_b_output,
        grad_first_gain,
        grad_first_shift,
    )
    every_done = reduce_every(attention_terms + dense_terms)
    attention_done = every_done[:9]
    dense_done = every_done[9:]
    return (
        mixed.astype(jnp.bfloat16).reshape(sequences, local_len, model_width),
        grad_tokens.reshape(sequences, local_len, model_width),
        attention_done[0],
        attention_done[1],
        attention_done[2],
        attention_done[3],
        attention_done[4],
        attention_done[5],
        attention_done[6],
        attention_done[7],
        attention_done[8],
        dense_done[0],
        dense_done[1],
        dense_done[2],
        dense_done[3],
        dense_done[4],
        dense_done[5],
    )


def solution(mesh):
    return jax.shard_map(
        body,
        mesh=mesh,
        in_specs=(
            P("dp", "seq", None),
            P("dp", None),
            P("dp", None),
            P("dp", None),
            P("dp", None),
            P("dp", None),
            P("dp"),
            P("dp"),
            P("dp"),
            P("dp"),
            P("dp"),
            P("dp", None),
            P("dp"),
            P("dp", None),
            P("dp"),
            P("dp"),
            P("dp"),
            P("dp", "seq", None),
        ),
        out_specs=(
            P("dp", "seq", None),
            P("dp", "seq", None),
            P("dp", None),
            P("dp", None),
            P("dp", None),
            P("dp", None),
            P("dp"),
            P("dp"),
            P("dp"),
            P("dp"),
            P("dp"),
            P("dp", None),
            P("dp"),
            P("dp", None),
            P("dp"),
            P("dp"),
            P("dp"),
        ),
        check_vma=False,
    )
```

profile of v0, /device:TPU:0, one launch (start us, length us, event | category | flops | bytes accessed | tf_op | source)
XLA Modules:
  0.0 1483.1 jit_solution(3374280511466156422)
XLA Ops:
  18.4 39.8 %all-reduce.18 = (bf16[768]{0:T(1024)(128)(2,1)S(1)}, bf16[768]{0:T(1024)(128)(2,1)S(1)}, bf16[768]{0:T(1024)(128)(2,1)}, bf16[768]{0:T(1024)(128)(2,1)}, bf16[7...) all-reduce(bf16[768]{0:T(1024)(128)(2,1)S(1)} %dynamic-update-slice, ...), channel_id=1, replica_groups=mesh['dp'=8,'seq'=4] {'dp'}, use_global_device_ids=true, to_apply=%add | all-reduce | flops 6144 | bytes 24576
  67.5 30.0 %all-gather.8.cloned.1.call-done = bf16[768,768]{1,0:T(8,128)(2,1)} async-done(((bf16[96,768]{1,0:T(8,128)(2,1)}), bf16[768,768]{1,0:T(8,128)(2,1)}) %all-gather.8.cloned.1.call-update) | async-done | bytes 1179664 | tf_op jit(solution)/shard_map/all_gather | solution.py:209
  107.3 32.9 %all-gather.10.cloned.1.call-done = bf16[768,768]{1,0:T(8,128)(2,1)} async-done(((bf16[96,768]{1,0:T(8,128)(2,1)}), bf16[768,768]{1,0:T(8,128)(2,1)}) %all-gather.10.cloned.1.call-update) | async-done | bytes 1179664 | tf_op jit(solution)/shard_map/all_gather | solution.py:210
  158.3 15.6 %all-to-all-done.1 = bf16[2,512,768]{1,0,2:T(2,128)(2,1)} async-done(((bf16[2,512,768]{1,0,2:T(2,128)(2,1)}), bf16[2,512,768]{1,0,2:T(2,128)(2,1)}, u32[]{:S(2)}, u32[]{:S(2)}) %all-to-all-start.1) | async-done | bytes 1572896 | tf_op jit(solution)/shard_map/all_to_all | solution.py:256
  178.3 193.5 %while.54 = (s32[]{:T(128)}, bf16[2,2048,192]{2,1,0:T(8,128)(2,1)}, f32[2,4,3,512,1]{3,2,1,4,0:T(4,128)S(1)}, bf16[2,2048,192]{1,2,0:T(8,128)(2,1)S(1)}, s32[2,2...) while((s32[]{:T(128)}, bf16[2,2048,192]{2,1,0:T(8,128)(2,1)}, ...), condition=%wide.region_5.6_spmd, body=%wide.region_0.5_spmd.sunk | while | flops 844200448 | bytes 56119792 | solution.py:271
  181.9 92.0 %while.57 = (s32[]{:T(128)}, bf16[4,512,192]{1,2,0:T(8,128)(2,1)S(1)}, f32[4,3,512,1]{2,1,3,0:T(4,128)S(1)}, s32[4]{0:T(128)S(1)}, s32[2048]{0:T(1024)S(1)}, /*i...) while((s32[]{:T(128)}, ...), condition=%wide.region_4.4_spmd, body=%wide.region_1.3_spmd.sunk | while | flops 844200448 | bytes 47911136 | solution.py:100
  279.0 91.2 %while.57 = (s32[]{:T(128)}, bf16[4,512,192]{1,2,0:T(8,128)(2,1)S(1)}, f32[4,3,512,1]{2,1,3,0:T(4,128)S(1)}, s32[4]{0:T(128)S(1)}, s32[2048]{0:T(1024)S(1)}, /*i...) while((s32[]{:T(128)}, ...), condition=%wide.region_4.4_spmd, body=%wide.region_1.3_spmd.sunk | while | flops 844200448 | bytes 47911136 | solution.py:100
  385.0 26.1 %all-gather = bf16[8,1,384]{2,1,0:T(2,128)(2,1)S(1)} all-gather(bf16[1,1,384]{2,1,0:T(2,128)(2,1)S(1)} %reshape.328), channel_id=1, replica_groups=mesh['dp'=8,'seq'=4] {'dp'}, dimensions={0}, use_global_device_ids=true | all-gather | bytes 6912 | tf_op jit(solution)/shard_map/all_gather | solution.py:219
  411.2 10.3 copy.92
  430.6 12.4 multiply_convert_fusion.1
  458.5 14.1 convert_reduce_fusion
  498.1 14.8 all-to-all-done.4
  517.5 298.2 %while.56 = (s32[]{:T(128)}, bf16[2,2048,192]{2,1,0:T(8,128)(2,1)}, bf16[2,2048,192]{1,2,0:T(8,128)(2,1)}, bf16[2,2048,192]{1,2,0:T(8,128)(2,1)}, bf16[2,2048,19...) while((s32[]{:T(128)}, bf16[2,2048,192]{2,1,0:T(8,128)(2,1)}, ...), condition=%wide.region_18.19_spmd, body=%wide.region_14.18_spmd.sunk | while | flops 2064448000 | bytes 207414256 | solution.py:338
  522.4 135.9 %while.58 = (s32[]{:T(128)}, f32[2048,3,64]{0,2,1:T(8,128)}, f32[2048,3,64]{0,2,1:T(8,128)}, bf16[4,512,192]{1,2,0:T(8,128)(2,1)}, s32[4]{0:T(128)S(1)}, /*index...) while((s32[]{:T(128)}, f32[2048,3,64]{0,2,1:T(8,128)}, ...), condition=%wide.region_17.17_spmd.clone, body=%wide.region_15.16_spmd.clone.sunk | while | flops 2063661568 | bytes 145088912 | solution.py:141
  671.2 135.8 %while.58 = (s32[]{:T(128)}, f32[2048,3,64]{0,2,1:T(8,128)}, f32[2048,3,64]{0,2,1:T(8,128)}, bf16[4,512,192]{1,2,0:T(8,128)(2,1)}, s32[4]{0:T(128)S(1)}, /*index...) while((s32[]{:T(128)}, f32[2048,3,64]{0,2,1:T(8,128)}, ...), condition=%wide.region_17.17_spmd.clone, body=%wide.region_15.16_spmd.clone.sunk | while | flops 2063661568 | bytes 145088912 | solution.py:141
  820.4 28.9 %all_to_all.132 = bf16[2,2048,192]{2,0,1:T(2,128)(2,1)} all-to-all(bf16[2,2048,192]{2,0,1:T(2,128)(2,1)S(1)} %copy.98), channel_id=1, replica_groups=mesh['dp'=8,'seq'=4] {'seq'}, dimensions={1} | all-to-all | bytes 3145728 | tf_op jit(solution)/shard_map/all_to_all | solution.py:342
  871.1 28.9 %all_to_all.133 = bf16[2,2048,192]{2,0,1:T(2,128)(2,1)} all-to-all(bf16[2,2048,192]{2,0,1:T(2,128)(2,1)S(1)} %copy.102), channel_id=1, replica_groups=mesh['dp'=8,'seq'=4] {'seq'}, dimensions={1} | all-to-all | bytes 3145728 | tf_op jit(solution)/shard_map/all_to_all | solution.py:344
  921.7 28.9 %all_to_all.134 = bf16[2,2048,192]{2,0,1:T(2,128)(2,1)} all-to-all(bf16[2,2048,192]{2,0,1:T(2,128)(2,1)S(1)} %copy.100), channel_id=1, replica_groups=mesh['dp'=8,'seq'=4] {'seq'}, dimensions={1} | all-to-all | bytes 3145728 | tf_op jit(solution)/shard_map/all_to_all | solution.py:343
  967.8 10.7 fusion.41
  980.4 10.4 fusion.38
  1007.9 67.1 %reduce-scatter.21.cloned.1.call-done = f32[96,768]{1,0:T(8,128)} async-done(((f32[768,768]{1,0:T(8,128)}), f32[96,768]{1,0:T(8,128)}) %reduce-scatter.21.cloned.1.call-update) | async-done | bytes 294928
  1076.8 164.2 %reduce-scatter.15.cloned.1.call-done = f32[96,3072]{1,0:T(8,128)} async-done(((f32[768,3072]{1,0:T(8,128)}), f32[96,3072]{1,0:T(8,128)}) %reduce-scatter.15.cloned.1.call-update) | async-done | bytes 1179664 | tf_op jit(solution)/shard_map/reduce_scatter | solution.py:162
  1243.1 163.7 %reduce-scatter.17.cloned.1.call-done = f32[384,768]{1,0:T(8,128)} async-done(((f32[3072,768]{1,0:T(8,128)}), f32[384,768]{1,0:T(8,128)}) %reduce-scatter.17.cloned.1.call-update) | async-done | bytes 1179664 | tf_op jit(solution)/shard_map/reduce_scatter | solution.py:164
  1411.5 35.6 %all-reduce.17 = (bf16[768]{0:T(1024)(128)(2,1)S(1)}, bf16[768]{0:T(1024)(128)(2,1)S(1)}, bf16[768]{0:T(1024)(128)(2,1)S(1)}, bf16[768]{0:T(1024)(128)(2,1)S(1)}...) all-reduce(f32[768]{0:T(1024)S(1)} %reduce_sum.184, ...), channel_id=6, replica_groups=mesh['dp'=8,'seq'=4] {'dp'}, use_global_device_ids=true, to_apply=%region_28.29.clone | all-reduce | flops 9216 | bytes 55296
  (629 shorter events, 703.5 us)
Async XLA Ops:
  7.3 50.9 %all-gather.12.cloned.1.call-start = ((), (), s32[]{:S(2)}) async-start(), calls=%async_computation.16 | async-start | bytes 1327104 | tf_op jit(solution)/shard_map/all_gather | solution.py:211
  9.2 88.3 %all-gather.8.cloned.1.call-start = ((), (), s32[]{:S(2)}) async-start(), calls=%async_computation.14 | async-start | bytes 1327104 | tf_op jit(solution)/shard_map/all_gather | solution.py:209
  10.9 129.3 %all-gather.10.cloned.1.call-start = ((), (), s32[]{:S(2)}) async-start(), calls=%async_computation.15 | async-start | bytes 1327104 | tf_op jit(solution)/shard_map/all_gather | solution.py:210
  12.6 411.9 %all-gather.14.cloned.1.call-start = ((), (), s32[]{:S(2)}) async-start(), calls=%async_computation.17 | async-start | bytes 1327104 | tf_op jit(solution)/shard_map/all_gather | solution.py:212
  14.3 416.3 %all-gather.16.cloned.1.call-start = ((), (), s32[]{:S(2)}) async-start(), calls=%async_computation.18 | async-start | bytes 5308416 | tf_op jit(solution)/shard_map/all_gather | solution.py:218
  63.9 39.8 %all-to-all-start.2 = ((bf16[2,512,768]{1,0,2:T(2,128)(2,1)}), bf16[2,512,768]{1,0,2:T(2,128)(2,1)S(1)}, u32[]{:S(2)}, u32[]{:S(2)}) async-start(bf16[2,512,768]{1,0,2:T(2,128)(2,1)} %copy.88), calls=%async_computation.2 | async-start | bytes 3145728 | tf_op jit(solution)/shard_map/all_to_all | solution.py:263
  103.7 45.7 %all-to-all-start = ((bf16[2,512,768]{1,0,2:T(2,128)(2,1)}), bf16[2,512,768]{1,0,2:T(2,128)(2,1)S(1)}, u32[]{:S(2)}, u32[]{:S(2)}) async-start(bf16[2,512,768]{1,0,2:T(2,128)(2,1)} %copy.82), calls=%async_computation | async-start | bytes 3145728 | tf_op jit(solution)/shard_map/all_to_all | solution.py:249
  149.4 24.5 %all-to-all-start.1 = ((bf16[2,512,768]{1,0,2:T(2,128)(2,1)}), bf16[2,512,768]{1,0,2:T(2,128)(2,1)}, u32[]{:S(2)}, u32[]{:S(2)}) async-start(bf16[2,512,768]{1,0,2:T(2,128)(2,1)} %copy.85), calls=%async_computation.1 | async-start | bytes 3145728 | tf_op jit(solution)/shard_map/all_to_all | solution.py:256
  153.7 289.3 %all-gather.18.cloned.1.call-start = ((), (), s32[]{:S(2)}) async-start(), calls=%async_computation.19 | async-start | bytes 5308416 | tf_op jit(solution)/shard_map/all_gather | solution.py:220
  377.6 33.5 %all-to-all-start.3 = ((bf16[2,2048,192]{2,0,1:T(2,128)(2,1)}), bf16[2,2048,192]{2,0,1:T(2,128)(2,1)}, u32[]{:S(2)}, u32[]{:S(2)}) async-start(bf16[2,2048,192]{2,0,1:T(2,128)(2,1)} %copy.91), calls=%async_computation.3 | async-start | bytes 4194304 | tf_op jit(solution)/shard_map/all_to_all | solution.py:272
  488.4 24.5 %all-to-all-start.4 = ((bf16[2,512,768]{1,0,2:T(2,128)(2,1)}), bf16[2,512,768]{1,0,2:T(2,128)(2,1)}, u32[]{:S(2)}, u32[]{:S(2)}) async-start(bf16[2,512,768]{1,0,2:T(2,128)(2,1)} %copy.93), calls=%async_computation.4 | async-start | bytes 3145728 | tf_op jit(solution)/shard_map/all_to_all | solution.py:335
  492.8 509.7 %reduce-scatter.13.cloned.1.call-start = ((), (), s32[]{:S(2)}) async-start(), calls=%async_computation.20 | async-start | bytes 2654208 | tf_op jit(solution)/shard_map/reduce_scatter | solution.py:156
  498.1 506.1 %reduce-scatter.19.cloned.1.call-start = ((), (), s32[]{:S(2)}) async-start(), calls=%async_computation.23 | async-start | bytes 2654208
  866.3 139.6 %reduce-scatter.23.cloned.1.call-start = ((), (), s32[]{:S(2)}) async-start(), calls=%async_computation.25 | async-start | bytes 2654208
  917.0 158.0 %reduce-scatter.21.cloned.1.call-start = ((), (), s32[]{:S(2)}) async-start(), calls=%async_computation.24 | async-start | bytes 2654208
  967.7 273.2 %reduce-scatter.15.cloned.1.call-start = ((), (), s32[]{:S(2)}) async-start(), calls=%async_computation.21 | async-start | bytes 10616832 | tf_op jit(solution)/shard_map/reduce_scatter | solution.py:162
  978.5 428.3 %reduce-scatter.17.cloned.1.call-start = ((), (), s32[]{:S(2)}) async-start(), calls=%async_computation.22 | async-start | bytes 10616832 | tf_op jit(solution)/shard_map/reduce_scatter | solution.py:164
  990.8 475.4 %all-reduce.23.cloned.1.call-start = ((), (), s32[]{:S(2)}) async-start(), calls=%async_computation.26 | async-start | bytes 3833856 | tf_op jit(solution)/shard_map/psum | solution.py:170
  1006.0 403.0 %copy-start.12 = (bf16[2,4,512,192]{2,0,3,1:T(2,128)(2,1)S(1)}, bf16[2,4,512,192]{2,0,3,1:T(2,128)(2,1)}, u32[]{:S(2)}) copy-start(bf16[2,4,512,192]{2,0,3,1:T(2,128)(2,1)} %copy-done.11) | copy-start | bytes 4718596
  1076.7 334.7 %copy-start.44 = (f32[768]{0:T(1024)S(1)}, f32[768]{0:T(1024)}, u32[]{:S(2)}) copy-start(f32[768]{0:T(1024)} %get-tuple-element.474) | copy-start | bytes 9220
  1076.7 334.7 %copy-start.45 = (f32[768]{0:T(1024)S(1)}, f32[768]{0:T(1024)}, u32[]{:S(2)}) copy-start(f32[768]{0:T(1024)} %get-tuple-element.362) | copy-start | bytes 9220
  1076.7 334.7 %copy-start.46 = (f32[3072]{0:T(1024)S(1)}, f32[3072]{0:T(1024)}, u32[]{:S(2)}) copy-start(f32[3072]{0:T(1024)} %get-tuple-element.498) | copy-start | bytes 36868
  1076.8 334.7 %copy-start.47 = (f32[768]{0:T(1024)S(1)}, f32[768]{0:T(1024)}, u32[]{:S(2)}) copy-start(f32[768]{0:T(1024)} %get-tuple-element.360) | copy-start | bytes 9220
  1076.8 334.7 %copy-start.48 = (f32[768]{0:T(1024)S(1)}, f32[768]{0:T(1024)}, u32[]{:S(2)}) copy-start(f32[768]{0:T(1024)} %get-tuple-element.365) | copy-start | bytes 9220
  (112 other events, 1730.9 us)
Sparse Core Ops, SparseCore 0:
  10.9 43.7 all-gather.11
  57.5 39.9 all-gather.7
  100.3 39.8 all-gather.9
  142.8 39.8 all-gather.13
  184.7 78.6 all-gather.15
  265.4 78.0 all-gather.17
  498.2 66.8 reduce-scatter.12
  866.5 65.3 reduce-scatter.18
  935.4 68.0 reduce-scatter.22
  1006.8 68.1 reduce-scatter.20
  1078.6 162.3 reduce-scatter.14
  1244.4 162.3 reduce-scatter.16
  1410.8 48.8 all-reduce.22
where the time goes:
time: 1490 us; the launch traced here: 1480 us
  waiting for transfers between devices  489 us (33%)
  matrix products  396 us (27%)
  blocking collectives  195 us (13%)
  local copies, waits for them, and re-layouts  176 us (12%)
  other arithmetic  161 us (11%)
  loops' own time  27.8 us (2%)
  starting transfers between devices  21 us (1%)
  between operations  17.3 us (1%)
    reduce_scatter x1, waiting for transfers between devices, reduce_every(): lax.psum_scatter(terms[9], 'dp', scatter_dimension=0, tiled=True)  164 us
    reduce_scatter x1, waiting for transfers between devices, reduce_every(): lax.psum_scatter(terms[11], 'dp', scatter_dimension=0, tiled=True)  164 us
    unnamed x2, blocking collectives  75.4 us
    dot_general x16, matrix products, scores_of(): jnp.einsum('qhd,khd->hqk', query_heads, key_heads, preferred_element_type...  72 us
    unnamed x16, waiting for transfers between devices  67.3 us
    reduce_sum x8, other arithmetic, one_block(): row_total = jnp.sum(exponent, axis=-1, keepdims=True)  55.3 us
    dot_general x8, matrix products, one_block(): jnp.einsum('hqk,khd->qhd', weights, value_heads, preferred_element_type=j...  53.9 us
    convert_element_type x8, other arithmetic, one_block(): grad_scores = (weights * (grad_weights - jnp.sum(weights * grad_weights,...  48.7 us
  transfers between devices with their start and end apart: 18, of which 7 were waited for; matrix products, arithmetic and copies ran while one was open for 45% of the time, Pallas kernels for 0%

commit v1 on v0

v1 whole, which is shorter than its diff:
```python
import jax
import jax.numpy as jnp
from jax import lax
from jax.experimental import pallas as pl
from jax.experimental.pallas import tpu as pltpu
from jax.sharding import Mesh
from jax.sharding import PartitionSpec as P

BLK = 256
BIG = -1.0e9

def dot_nt(a, b):
    return lax.dot_general(a, b, (((1,), (1,)), ((), ())), preferred_element_type=jnp.float32)

def dot_nn(a, b):
    return jnp.dot(a, b, preferred_element_type=jnp.float32)

def half_lanes(rows):
    return lax.broadcasted_iota(jnp.int32, (rows, 128), 1) < 64

def part_rows(place_ref, part, rows):
    return pl.ds(pl.multiple_of(place_ref[part], 128), rows)

def forward_kernel(place_ref, start_ref, count_ref, qkv_ref, ohq_ref, nohk_ref, ctx_ref, lse_ref, q2, k2, vt, acc, top, tot):
    length = qkv_ref.shape[0]
    blocks = length // BLK
    part = length // 4
    low = half_lanes(part)
    for b in range(4):
        src = part_rows(place_ref, b, part)
        dst = slice(b * part, (b + 1) * part)
        q, k = qkv_ref[src, 0:128], qkv_ref[src, 128:256]
        ohq, nohk = ohq_ref[dst, :], nohk_ref[dst, :]
        q2[0, dst, :] = jnp.where(low, q, ohq)
        q2[1, dst, :] = jnp.where(low, ohq, q)
        k2[0, dst, :] = jnp.where(low, k, nohk)
        k2[1, dst, :] = jnp.where(low, nohk, k)
        vt[:, dst] = qkv_ref[src, 256:384].T
    lse_ref[...] = jnp.zeros_like(lse_ref)

    def row(qb, _):
        qs = pl.ds(pl.multiple_of(qb * BLK, BLK), BLK)
        acc[...] = jnp.zeros_like(acc)
        top[...] = jnp.full_like(top, -1.0e30)
        tot[...] = jnp.zeros_like(tot)
        start, count = start_ref[qb], count_ref[qb]

        def tiles(first, number):
            spans = [pl.ds(pl.multiple_of(first + i * BLK, 128), BLK) for i in range(number)]
            for h in range(2):
                rows = slice(64 * h, 64 * h + 64)
                sts = [dot_nt(k2[h, ks, :], q2[h, qs, :]) for ks in spans]
                before = top[h : h + 1, :]
                after = before
                for st in sts:
                    after = jnp.maximum(after, jnp.max(st, axis=0, keepdims=True))
                alpha = jnp.exp(before - after)
                total = tot[h : h + 1, :] * alpha
                result = acc[rows, :] * alpha
                for ks, st in zip(spans, sts):
                    p = jnp.exp(st - after)
                    total = total + jnp.sum(p, axis=0, keepdims=True)
                    result = result + dot_nn(vt[rows, ks], p.astype(jnp.bfloat16))
                top[h : h + 1, :] = after
                tot[h : h + 1, :] = total
                acc[rows, :] = result

        def two(i, _):
            tiles(start + i * (2 * BLK), 2)
            return 0

        lax.fori_loop(0, count // 2, two, 0)

        @pl.when(count % 2 == 1)
        def _():
            tiles(start + (count - 1) * BLK, 1)

        for h in range(2):
            rows = slice(64 * h, 64 * h + 64)
            total = tot[h : h + 1, :]
            acc[rows, :] = acc[rows, :] / total
            lse_ref[h : h + 1, qs] = top[h : h + 1, :] + jnp.log(total)
        where = pl.ds(pl.multiple_of(place_ref[qb * BLK // part] + qb * BLK % part, BLK), BLK)
        ctx_ref[where, :] = acc[...].T.astype(jnp.bfloat16)
        return 0

    lax.fori_loop(0, blocks, row, 0)

def attention(place, start, count, qkv, ohq, nohk):
    length, width = qkv.shape
    pairs = width // 384
    return pl.pallas_call(
        forward_kernel,
        out_shape=(
            jax.ShapeDtypeStruct((length, pairs * 128), jnp.bfloat16),
            jax.ShapeDtypeStruct((pairs * 8, length), jnp.float32),
        ),
        grid_spec=pltpu.PrefetchScalarGridSpec(
            num_scalar_prefetch=3,
            grid=(pairs,),
            in_specs=[
                pl.BlockSpec((length, 384), lambda p, *_: (0, p)),
                pl.BlockSpec((length, 128), lambda p, *_: (0, 0)),
                pl.BlockSpec((length, 128), lambda p, *_: (0, 0)),
            ],
            out_specs=[
                pl.BlockSpec((length, 128), lambda p, *_: (0, p)),
                pl.BlockSpec((8, length), lambda p, *_: (p, 0)),
            ],
            scratch_shapes=[
                pltpu.VMEM((2, length, 128), jnp.bfloat16),
                pltpu.VMEM((2, length, 128), jnp.bfloat16),
                pltpu.VMEM((128, length), jnp.bfloat16),
                pltpu.VMEM((128, BLK), jnp.float32),
                pltpu.VMEM((8, BLK), jnp.float32),
                pltpu.VMEM((8, BLK), jnp.float32),
            ],
        ),
        compiler_params=pltpu.CompilerParams(dimension_semantics=("arbitrary",), vmem_limit_bytes=60 << 20),
        cost_estimate=pl.CostEstimate(flops=pairs * 8_000_000_000, bytes_accessed=pairs * 3_000_000, transcendentals=pairs * 4_000_000),
        name="attention_forward",
    )(place, start, count, qkv, ohq, nohk)

def backward_kernel(place_ref, start_ref, count_ref, qkv_ref, ctx_ref, do_ref, lse_ref, ohq_ref, nohk_ref, out_ref, q2, k2, q0, d0, v0, kt, dk, dv, dqt, delta):
    length = qkv_ref.shape[0]
    blocks = length // BLK
    part = length // 4
    low = half_lanes(part)
    for b in range(4):
        src = part_rows(place_ref, b, part)
        dst = slice(b * part, (b + 1) * part)
        q, k, do = qkv_ref[src, 0:128], qkv_ref[src, 128:256], do_ref[src, :]
        zero = jnp.zeros_like(q)
        ohq, nohk = ohq_ref[dst, :], nohk_ref[dst, :]
        q2[0, dst, :] = jnp.where(low, q, ohq)
        q2[1, dst, :] = jnp.where(low, ohq, q)
        k2[0, dst, :] = jnp.where(low, k, nohk)
        k2[1, dst, :] = jnp.where(low, nohk, k)
        q0[0, dst, :] = jnp.where(low, q, zero)
        q0[1, dst, :] = jnp.where(low, zero, q)
        d0[0, dst, :] = jnp.where(low, do, zero)
        d0[1, dst, :] = jnp.where(low, zero, do)
        v0[dst, :] = qkv_ref[src, 256:384]
        kt[:, dst] = k.T
        prod = (do.astype(jnp.float32) * ctx_ref[src, :].astype(jnp.float32)).T
        delta[0:1, dst] = jnp.sum(prod[0:64], axis=0, keepdims=True)
        delta[1:2, dst] = jnp.sum(prod[64:128], axis=0, keepdims=True)
    dk[...] = jnp.zeros_like(dk)
    dv[...] = jnp.zeros_like(dv)
    dqt[...] = jnp.zeros_like(dqt)

    def row(qb, _):
        qs = pl.ds(pl.multiple_of(qb * BLK, BLK), BLK)
        start, count = start_ref[qb], count_ref[qb]

        def tiles(first, number):
            spans = [pl.ds(pl.multiple_of(first + i * BLK, 128), BLK) for i in range(number)]
            for h in range(2):
                rows = slice(64 * h, 64 * h + 64)
                for ks in spans:
                    st = dot_nt(k2[h, ks, :], q2[h, qs, :])
                    w = jnp.exp(st - lse_ref[h : h + 1, qs])
                    gw = dot_nt(v0[ks, :], d0[h, qs, :])
                    ds = (w * (gw - delta[h : h + 1, qs])).astype(jnp.bfloat16)
                    dv[ks, :] += dot_nn(w.astype(jnp.bfloat16), d0[h, qs, :])
                    dk[ks, :] += dot_nn(ds, q0[h, qs, :])
                    dqt[rows, qs] += dot_nn(kt[rows, ks], ds)

        def two(i, _):
            tiles(start + i * (2 * BLK), 2)
            return 0

        lax.fori_loop(0, count // 2, two, 0)

        @pl.when(count % 2 == 1)
        def _():
            tiles(start + (count - 1) * BLK, 1)
        return 0

    lax.fori_loop(0, blocks, row, 0)
    for b in range(4):
        dst = part_rows(place_ref, b, part)
        src = slice(b * part, (b + 1) * part)
        out_ref[dst, 0:128] = (dqt[:, src].T * 0.125).astype(jnp.bfloat16)
        out_ref[dst, 128:256] = dk[src, :].astype(jnp.bfloat16)
        out_ref[dst, 256:384] = dv[src, :].astype(jnp.bfloat16)

def attention_back(place, start, count, qkv, ctx, do, lse, ohq, nohk):
    length, width = qkv.shape
    pairs = width // 384
    half = lambda: pltpu.VMEM((2, length, 128), jnp.bfloat16)
    return pl.pallas_call(
        backward_kernel,
        out_shape=jax.ShapeDtypeStruct((length, width), jnp.bfloat16),
        grid_spec=pltpu.PrefetchScalarGridSpec(
            num_scalar_prefetch=3,
            grid=(pairs,),
            in_specs=[
                pl.BlockSpec((length, 384), lambda p, *_: (0, p)),
                pl.BlockSpec((length, 128), lambda p, *_: (0, p)),
                pl.BlockSpec((length, 128), lambda p, *_: (0, p)),
                pl.BlockSpec((8, length), lambda p, *_: (p, 0)),
                pl.BlockSpec((length, 128), lambda p, *_: (0, 0)),
                pl.BlockSpec((length, 128), lambda p, *_: (0, 0)),
            ],
            out_specs=pl.BlockSpec((length, 384), lambda p, *_: (0, p)),
            scratch_shapes=[
                half(), half(), half(), half(),
                pltpu.VMEM((length, 128), jnp.bfloat16),
                pltpu.VMEM((128, length), jnp.bfloat16),
                pltpu.VMEM((length, 128), jnp.float32),
                pltpu.VMEM((length, 128), jnp.float32),
                pltpu.VMEM((128, length), jnp.float32),
                pltpu.VMEM((8, length), jnp.float32),
            ],
        ),
        compiler_params=pltpu.CompilerParams(dimension_semantics=("arbitrary",), vmem_limit_bytes=60 << 20),
        cost_estimate=pl.CostEstimate(flops=pairs * 20_000_000_000, bytes_accessed=pairs * 5_000_000, transcendentals=pairs * 4_000_000),
        name="attention_backward",
    )(place, start, count, qkv, ctx, do, lse, ohq, nohk)

def masks_of(segments):
    length = segments.shape[0]
    grid = segments.reshape(length // BLK, BLK)
    lo, hi = grid[:, 0], grid[:, -1]
    below = jnp.sum((segments[None, :] < lo[:, None]).astype(jnp.int32), axis=1)
    upto = jnp.sum((segments[None, :] <= hi[:, None]).astype(jnp.int32), axis=1)
    start = below // 128 * 128
    count = (upto - start + BLK - 1) // BLK
    start = jnp.minimum(start, length - count * BLK)
    lane = jnp.arange(128, dtype=jnp.int32) % 64
    same = lane[None, :] == segments[:, None]
    ohq = same.astype(jnp.bfloat16)
    nohk = jnp.where(jnp.logical_and(lane[None, :] < 4, jnp.logical_not(same)), BIG, 0.0).astype(jnp.bfloat16)
    return start, count, ohq, nohk


HD = 64
EPS = 1e-12
ROOT_HALF = 0.7071067811865476
INV_ROOT_TAU = 0.3989422804014327


def lowered(piece):
    return piece.astype(jnp.bfloat16)


def widen(piece):
    return piece.astype(jnp.float32)


def matmul(left, right):
    return jnp.dot(left, right, preferred_element_type=jnp.float32)


def matmul_tn(left, right):
    return lax.dot_general(
        left, right, (((0,), (0,)), ((), ())), preferred_element_type=jnp.float32
    )


def matmul_nt(left, right):
    return lax.dot_general(
        left, right, (((1,), (1,)), ((), ())), preferred_element_type=jnp.float32
    )


def normalize(hidden, norm_gain, norm_shift):
    centred = hidden - jnp.mean(hidden, axis=-1, keepdims=True)
    reciprocal = lax.rsqrt(jnp.mean(centred * centred, axis=-1, keepdims=True) + EPS)
    normed = centred * reciprocal
    return (normed * norm_gain + norm_shift, normed, reciprocal)


def normalize_back(upstream, normed, reciprocal, norm_gain):
    scaled = upstream * norm_gain
    result = reciprocal * (
        scaled
        - jnp.mean(scaled, axis=-1, keepdims=True)
        - normed * jnp.mean(scaled * normed, axis=-1, keepdims=True)
    )
    return (result, jnp.sum(upstream * normed, axis=0), jnp.sum(upstream, axis=0))


def gelu_value(values_in):
    return 0.5 * values_in * (1.0 + lax.erf(values_in * ROOT_HALF))


def gelu_slope(values_in):
    return (
        0.5 * (1.0 + lax.erf(values_in * ROOT_HALF))
        + values_in * jnp.exp(-0.5 * values_in * values_in) * INV_ROOT_TAU
    )


def shift(piece, axis, step):
    size = lax.axis_size(axis)
    return lax.ppermute(piece, axis, [(i, (i + step) % size) for i in range(size)])


def swap(piece, axis):
    return lax.ppermute(piece, axis, [(0, 1), (1, 0)])


def pick(piece, index, axis=0):
    return lax.dynamic_index_in_dim(piece, index, axis, keepdims=False)


def in_order(first_is_zero, own, other, axis):
    return jnp.where(
        first_is_zero,
        jnp.concatenate([own, other], axis),
        jnp.concatenate([other, own], axis),
    )


def collect(piece):
    size_z, size_x = lax.axis_size("z"), lax.axis_size("x")
    z, x = lax.axis_index("z"), lax.axis_index("x")
    along_z = [piece] + [shift(piece, "z", k) for k in range(1, size_z)]
    whole = jnp.zeros((size_z, size_x) + piece.shape, piece.dtype)
    zeros = (0,) * piece.ndim
    for j in range(size_x):
        for k in range(size_z):
            arrived = along_z[k] if j == 0 else shift(along_z[k], "x", j)
            place = ((z - k) % size_z, (x - j) % size_x) + zeros
            whole = lax.dynamic_update_slice(whole, arrived[None, None], place)
    return whole.reshape((size_z * size_x,) + piece.shape)


def reduce_owned(terms):
    size_z, size_x = lax.axis_size("z"), lax.axis_size("x")
    z, x = lax.axis_index("z"), lax.axis_index("x")
    terms = terms.reshape((size_z, size_x) + terms.shape[1:])
    total = widen(pick(terms, x, 1))
    for j in range(1, size_x):
        total = total + widen(shift(pick(terms, (x + j) % size_x, 1), "x", j))
    terms = lowered(total)
    total = widen(pick(terms, z))
    for k in range(1, size_z):
        total = total + widen(shift(pick(terms, (z + k) % size_z), "z", k))
    terms = lowered(total)
    return widen(terms) + widen(swap(terms, "y"))


def body(
    tokens,
    segment_ids,
    w_query,
    w_key,
    w_value,
    w_output,
    b_query,
    b_value,
    b_output,
    first_gain,
    first_shift,
    w_inner,
    b_inner,
    w_outer,
    b_outer,
    second_gain,
    second_shift,
    cotangent,
):
    core, y = lax.axis_index("core"), lax.axis_index("y")
    shards = lax.axis_size("z") * lax.axis_size("x")
    sequences, part, width = tokens.shape
    half = width // 2
    pairs = half // 128
    hidden = w_inner.shape[1]
    local = 2 * part
    own_rows = w_query.shape[0]
    unit_half = hidden // shards // 2

    def columns(matrix):
        return lowered(lax.dynamic_slice_in_dim(matrix, core * half, half, 1))

    vectors = (b_query, b_value, b_output, first_gain, first_shift, b_inner, b_outer, second_gain, second_shift)
    flat = jnp.concatenate([lowered(v) for v in vectors])
    lanes = 3 * half
    extra = -(-flat.shape[0] // lanes)
    flat = jnp.pad(flat, (0, extra * lanes - flat.shape[0])).reshape(extra, lanes)
    weights = jnp.stack([columns(w).reshape(own_rows, pairs, 128) for w in (w_query, w_key, w_value)], axis=2)
    early = collect(jnp.concatenate([weights.reshape(own_rows, lanes), flat], axis=0))

    mine = pick(tokens, y)
    arrived = swap(pick(tokens, 1 - y), "y")
    mine_other, arrived_other = swap(mine, "core"), swap(arrived, "core")
    inputs_all = jnp.concatenate([mine, arrived, mine_other, arrived_other], axis=0)
    inputs = jnp.concatenate([mine, arrived], axis=0)

    inner_piece = lowered(pick(w_inner.reshape(own_rows, shards, 2, unit_half), core, 2)).reshape(own_rows, hidden // 2)
    late = collect(jnp.concatenate([columns(w_output), inner_piece], axis=1)).reshape(width, half + hidden // 2)
    outer_own = collect(lowered(lax.dynamic_slice_in_dim(w_outer, core * unit_half, unit_half, 0))).reshape(hidden // 2, width)
    output_own, inner_own = late[:, :half], late[:, half:]
    output_other, inner_other, outer_other = swap(output_own, "core"), swap(inner_own, "core"), swap(outer_own, "core")
    full_output = in_order(core == 0, output_own, output_other, 1)
    cotangent_mine = pick(cotangent, y)
    cotangent_arrived = swap(pick(cotangent, 1 - y), "y")

    full_early = early[:, :own_rows].reshape(width, lanes)
    flat_all = early[:, own_rows:].reshape(shards, extra * lanes)
    sizes = [v.shape[0] for v in vectors]
    gathered, at = [], 0
    for size in sizes:
        gathered.append(flat_all[:, at : at + size].reshape(shards * size))
        at += size
    bias_query, bias_value, bias_output, gain_first, shift_first, bias_inner, bias_outer, gain_second, shift_second = [
        widen(v) for v in gathered
    ]
    heads_query = lax.dynamic_slice_in_dim(bias_query, core * half, half).reshape(pairs, 1, 128)
    heads_value = lax.dynamic_slice_in_dim(bias_value, core * half, half).reshape(pairs, 1, 128)
    bias_all = jnp.concatenate([heads_query, jnp.zeros_like(heads_query), heads_value], axis=1).reshape(lanes)
    scale = jnp.tile(jnp.concatenate([jnp.full((128,), HD ** (-0.5)), jnp.ones((256,))]), pairs)
    projected = lowered((matmul(inputs_all, full_early) + bias_all) * scale)

    start, count, mark_query, mark_key = masks_of(pick(segment_ids, y))
    spot = jnp.arange(4, dtype=jnp.int32)
    place = ((spot % 2 != core) * 2 + (spot // 2 != y) * 1) * part
    context_heads, logsum = attention(place, start, count, projected, mark_query, mark_key)
    context = in_order(core == 0, context_heads[:local], swap(context_heads[local:], "core"), 1)

    attended = matmul(context, full_output) + bias_output
    first, first_normed, first_recip = normalize(widen(inputs) + attended, gain_first, shift_first)
    first_low = lowered(first)
    biases = bias_inner.reshape(shards, 2, unit_half)
    halves = ((inner_own, outer_own, pick(biases, core, 1)), (inner_other, outer_other, pick(biases, 1 - core, 1)))
    outer, kept = bias_outer, []
    for inner_weight, outer_weight, bias in halves:
        inner = matmul(first_low, inner_weight) + bias.reshape(hidden // 2)
        active = lowered(gelu_value(inner))
        outer = outer + matmul(active, outer_weight)
        kept.append((inner, active))
    mixed, second_normed, second_recip = normalize(first + outer, gain_second, shift_second)
    mixed = lowered(mixed)

    upstream = widen(jnp.concatenate([cotangent_mine, cotangent_arrived], axis=0))
    pre_second, grad_second_gain, grad_second_shift = normalize_back(upstream, second_normed, second_recip, gain_second)
    grad_outer = lowered(pre_second)
    grad_b_outer = jnp.sum(widen(grad_outer), axis=0)
    grad_first, inner_grads, outer_grads, bias_grads = pre_second, [], [], []
    for (inner, active), (inner_weight, outer_weight, _) in zip(kept, halves):
        grad_inner = lowered(matmul_nt(grad_outer, outer_weight) * gelu_slope(inner))
        outer_grads.append(lowered(matmul_tn(active, grad_outer)))
        inner_grads.append(lowered(matmul_tn(first_low, grad_inner)))
        bias_grads.append(jnp.sum(widen(grad_inner), axis=0).reshape(shards, 1, unit_half))
        grad_first = grad_first + matmul_nt(grad_inner, inner_weight)
    grad_b_inner = in_order(core == 0, bias_grads[0], bias_grads[1], 1).reshape(hidden)
    pre_first, grad_first_gain, grad_first_shift = normalize_back(grad_first, first_normed, first_recip, gain_first)
    grad_attended = lowered(pre_first)
    grad_b_output = jnp.sum(widen(grad_attended), axis=0)
    grad_w_output = lowered(matmul_tn(context, grad_attended))
    grad_context = lowered(matmul_nt(grad_attended, full_output))
    context_mine = lax.dynamic_slice_in_dim(grad_context, core * half, half, 1)
    context_other = lax.dynamic_slice_in_dim(grad_context, (1 - core) * half, half, 1)
    upstream_heads = jnp.concatenate([context_mine, swap(context_other, "core")], axis=0)

    def core_sum(own, other):
        return lowered(widen(own) + widen(swap(other, "core")))

    outer_term = core_sum(*outer_grads)
    inner_term = core_sum(*inner_grads)
    output_term = core_sum(
        lax.dynamic_slice_in_dim(grad_w_output, core * half, half, 1),
        lax.dynamic_slice_in_dim(grad_w_output, (1 - core) * half, half, 1),
    )
    outer_done = reduce_owned(outer_term.reshape(shards, unit_half, width))
    late_done = reduce_owned(jnp.concatenate([output_term, inner_term], axis=1).reshape(shards, own_rows, half + hidden // 2))

    grads = attention_back(place, start, count, projected, context_heads, upstream_heads, logsum, mark_query, mark_key)
    grad_early = lowered(matmul_tn(inputs_all, grads))
    partial = matmul_nt(grads, full_early)
    sums = jnp.sum(widen(grads), axis=0).reshape(pairs, 3, 128)
    blank = jnp.zeros((width,), jnp.float32)
    grad_b_query = lax.dynamic_update_slice(blank, sums[:, 0].reshape(half), (core * half,))
    grad_b_value = lax.dynamic_update_slice(blank, sums[:, 2].reshape(half), (core * half,))
    vector_grads = (
        grad_b_query,
        grad_b_value,
        grad_b_output,
        grad_first_gain,
        grad_first_shift,
        grad_b_inner,
        grad_b_outer,
        grad_second_gain,
        grad_second_shift,
    )
    flat_grads = jnp.concatenate([v.reshape(shards, -1) for v in vector_grads], axis=1)
    flat_grads = jnp.pad(flat_grads, ((0, 0), (0, extra * lanes - flat_grads.shape[1])))
    early_term = jnp.concatenate(
        [grad_early.reshape(shards, own_rows, lanes), lowered(flat_grads).reshape(shards, extra, lanes)], axis=1
    )
    early_done = reduce_owned(early_term)

    grad_inputs = pre_first + partial[:local] + widen(swap(lowered(partial[local:]), "core"))
    returned = widen(swap(lowered(grad_inputs[part:]), "y"))
    grad_tokens = in_order(y == 0, grad_inputs[None, :part], returned[None], 0)
    mixed_out = in_order(y == 0, mixed[None, :part], swap(mixed[part:], "y")[None], 0)

    def both(piece):
        return widen(swap(lowered(piece), "core"))

    early_matrix = early_done[:own_rows]
    early_full = in_order(
        core == 0, early_matrix.reshape(own_rows, pairs, 3, 128)[None], both(early_matrix).reshape(own_rows, pairs, 3, 128)[None], 0
    )
    early_full = early_full.transpose(3, 1, 0, 2, 4).reshape(3, own_rows, width)
    late_other = both(late_done)
    output_full = in_order(core == 0, late_done[:, :half], late_other[:, :half], 1)
    inner_full = in_order(
        core == 0,
        late_done[:, half:].reshape(own_rows, shards, 1, unit_half),
        late_other[:, half:].reshape(own_rows, shards, 1, unit_half),
        2,
    ).reshape(own_rows, hidden)
    outer_full = in_order(core == 0, outer_done, both(outer_done), 0)
    vector_part = early_done[own_rows:]
    vector_sums = (vector_part + swap(vector_part, "core")).reshape(extra * lanes)
    out_vectors, at = [], 0
    for size in sizes:
        out_vectors.append(vector_sums[at : at + size])
        at += size
    (
        done_b_query,
        done_b_value,
        done_b_output,
        done_first_gain,
        done_first_shift,
        done_b_inner,
        done_b_outer,
        done_second_gain,
        done_second_shift,
    ) = out_vectors
    return (
        mixed_out,
        grad_tokens,
        early_full[0],
        early_full[1],
        early_full[2],
        output_full,
        done_b_query,
        done_b_value,
        done_b_output,
        done_first_gain,
        done_first_shift,
        inner_full,
        done_b_inner,
        outer_full,
        done_b_outer,
        done_second_gain,
        done_second_shift,
    )


def solution(mesh):
    outer, inner = mesh.devices.shape
    size_z = 1
    while size_z * size_z < outer:
        size_z *= 2
    split = Mesh(mesh.devices.reshape(size_z, outer // size_z, inner // 2, 2), ("z", "x", "y", "core"))
    dp, seq = ("z", "x"), ("y", "core")
    activation, matrix, vector = P(dp, seq, None), P(dp, None), P(dp)
    return jax.shard_map(
        body,
        mesh=split,
        in_specs=(
            activation,
            matrix,
            matrix,
            matrix,
            matrix,
            matrix,
            vector,
            vector,
            vector,
            vector,
            vector,
            matrix,
            vector,
            matrix,
            vector,
            vector,
            vector,
            activation,
        ),
        out_specs=(
            activation,
            activation,
            matrix,
            matrix,
            matrix,
            matrix,
            vector,
            vector,
            vector,
            vector,
            vector,
            matrix,
            vector,
            matrix,
            vector,
            vector,
            vector,
        ),
        check_vma=False,
    )
```

time: 1490 us -> 615 us (0.41)
  waiting for transfers between devices: 489 us -> 139 us
  matrix products: 396 us -> 103 us
  blocking collectives: 195 us -> 0 us
  Pallas kernels: 0 us -> 131 us
  other arithmetic: 161 us -> 50.2 us
  local copies, waits for them, and re-layouts: 176 us -> 118 us
  starting transfers between devices: 21 us -> 60.9 us
  loops' own time: 27.8 us -> 0 us
  between operations: 17.3 us -> 2.26 us
    reduce_scatter x3 -> x0, waiting for transfers between devices: 328 us -> none  [the longest x1 164 us: reduce_every(): lax.psum_scatter(terms[9], 'dp', scatter_dimension=0, tiled=True)]
    dot_general x56 -> x0, matrix products: 288 us -> none  [the longest x16 72 us: scores_of(): jnp.einsum('qhd,khd->hqk', query_heads, key_heads, preferred_element_type...]
    ppermute x0 -> x55, waiting for transfers between devices: none -> 139 us  [the longest x33 126 us: shift(): lax.ppermute(piece, axis, [(i, (i + step) % size) for i in range(size)])]
    pallas_call x0 -> x2, Pallas kernels: none -> 131 us  [the longest x1 70.7 us: attention_back(): pl.pallas_call(backward_kernel, out_shape=jax.ShapeDtypeStruct((length, w...]
    all_to_all x3 -> x0, blocking collectives: 86.8 us -> none  [the longest x1 28.9 us: body(): lax.all_to_all(head_grads[0], 'seq', split_axis=1, concat_axis=2, tiled=T...]
    unnamed x2 -> x0, blocking collectives: 75.4 us -> none
    convert_element_type x27 -> x2, other arithmetic: 70.8 us -> 2.28 us  [the longest x1 1.14 us: masks_of(): jnp.where(jnp.logical_and(lane[None, :] < 4, jnp.logical_not(same)), BIG,...]
    unnamed x16 -> x0, waiting for transfers between devices: 67.3 us -> none
  transfers between devices with their start and end apart: 18 -> 55, of which waited for: 7 -> 19; matrix products, arithmetic and copies ran while one was open for 45% -> 33% of each run, Pallas kernels for 0% -> 22%
where the time goes in v1:
time: 615 us; the launch traced here: 605 us
  waiting for transfers between devices  139 us (23%)
  Pallas kernels  131 us (21%)
  local copies, waits for them, and re-layouts  118 us (19%)
  matrix products  103 us (17%)
  starting transfers between devices  60.9 us (10%)
  other arithmetic  50.2 us (8%)
    ppermute x33, waiting for transfers between devices, shift(): lax.ppermute(piece, axis, [(i, (i + step) % size) for i in range(size)])  126 us
    pallas_call x1, Pallas kernels, attention_back(): pl.pallas_call(backward_kernel, out_shape=jax.ShapeDtypeStruct((length, w...  70.7 us
    pallas_call x1, Pallas kernels, attention(): pl.pallas_call(forward_kernel, out_shape=(jax.ShapeDtypeStruct((length, p...  60.2 us
    ppermute x33, starting transfers between devices, shift(): lax.ppermute(piece, axis, [(i, (i + step) % size) for i in range(size)])  52.1 us
    dot_general x6, matrix products, matmul(): return jnp.dot(left, right, preferred_element_type=jnp.float32)  36.7 us
    dot_general x6, matrix products, matmul_nt(): lax.dot_general(left, right, (((1,), (1,)), ((), ())), preferred_element_...  35.1 us
    dot_general x6, matrix products, matmul_tn(): lax.dot_general(left, right, (((0,), (0,)), ((), ())), preferred_element_...  31.7 us
    dynamic_update_slice x23, local copies, waits for them, and re-layouts, collect(): whole = lax.dynamic_update_slice(whole, arrived[None, None], place)  22.5 us
  transfers between devices with their start and end apart: 55, of which 19 were waited for; matrix products, arithmetic and copies ran while one was open for 33% of the time, Pallas kernels for 22%

profile of v1, /device:TPU:0, one launch (start us, length us, event | category | flops | bytes accessed | tf_op | source)
XLA Modules:
  0.0 604.8 jit_solution(8677593160798432772)
XLA Ops:
  54.4 15.4 %collective-permute-done.19 = bf16[192,768]{1,0:T(8,128)(2,1)S(1)} collective-permute-done((bf16[192,768]{1,0:T(8,128)(2,1)S(1)}, bf16[192,768]{1,0:T(8,128)(2,1)S(1)}, u32[]{:S(2)}, u32[]{:S(2)}) %collective-permute-start.19) | collective-permute-done | bytes 294944 | tf_op jit(solution)/shard_map/ppermute | solution.py:298
  73.1 14.4 %collective-permute-done.20 = bf16[192,768]{1,0:T(8,128)(2,1)S(1)} collective-permute-done((bf16[192,768]{1,0:T(8,128)(2,1)S(1)}, bf16[192,768]{1,0:T(8,128)(2,1)S(1)}, u32[]{:S(2)}, u32[]{:S(2)}) %collective-permute-start.20) | collective-permute-done | bytes 294944 | tf_op jit(solution)/shard_map/ppermute | solution.py:298
  144.0 6.2 %collective-permute-done.16 = bf16[96,1920]{1,0:T(8,128)(2,1)S(1)} collective-permute-done((bf16[96,1920]{1,0:T(8,128)(2,1)}, bf16[96,1920]{1,0:T(8,128)(2,1)S(1)}, u32[]{:S(2)}, u32[]{:S(2)}) %collective-permute-start.16) | collective-permute-done | bytes 368672 | tf_op jit(solution)/shard_map/ppermute | solution.py:298
  154.1 8.7 %multiply_convert_fusion.qkv_ref = bf16[2048,1152]{1,0:T(8,128)(2,1)} fusion(bf16[768,1152]{1,0:T(8,128)(2,1)} %bitcast.182, f32[1152]{0:T(1024)} %mul.192, f32[1152]{0:T(1024)} %add.460, bf16[512,768]{0,1:T(8,128)(2,1)S(1)} %collective-permute-done.2, bf16[512,768]{0,1:T(8,128)(2,1)} %collective-permute-done.1, bf16[512,768]{0,1:T(8,128)(2,1)} %collective-permute-done, ...), kind=kOutput, calls=%fused_computation.3 | convolution fusion | flops 3643539456 | bytes 9643008 | tf_op jit(solution)/shard_map/dot_general | solution.py:253
  162.8 60.2 %attention_forward.1 = (bf16[2048,384]{1,0:T(8,128)(2,1)}, f32[24,2048]{1,0:T(8,128)}) custom-call(s32[4]{0:T(128)} %fusion.40.place_ref, s32[8]{0:T(128)} %get-tuple-element.163.start_ref, s32[8]{0:T(128)} %get-tuple-element.164.count_ref, bf16[2048,1152]{1,0:T(8,128)(2,1)} %multiply_convert_fusion.qkv_ref, bf16[2048,128]{1,0:T(8,128)(2,1)} %compare_convert_fusion.ohq_ref, ...), custom_call_target="tpu_custom_call" | custom-call | flops 24000000000 | bytes 9000000 | tf_op jit(solution)/shard_map/attention_forward/pallas_call | solution.py:92
  246.1 6.3 %multiply_convert_fusion.1 = (bf16[1024,1536]{1,0:T(8,128)(2,1)S(1)}, f32[1024,1536]{1,0:T(8,128)S(1)}) fusion(f32[1536]{0:T(1024)S(1)} %add.479, bf16[1024,768]{0,1:T(8,128)(2,1)S(1)} %fusion.21, bf16[768,1536]{1,0:T(8,128)(2,1)} %collective-permute-done.26), kind=kOutput, calls=%fused_computation.18 | convolution fusion | flops 2425356288 | bytes 13375488 | tf_op jit(solution)/shard_map/dot_general | solution.py:253
  252.4 7.2 %fusion.62 = f32[1024,768]{0,1:T(8,128)} fusion(bf16[1024,1536]{1,0:T(8,128)(2,1)S(1)} %get-tuple-element.211, bf16[1536,768]{1,0:T(8,128)(2,1)} %collective-permute-done.27), kind=kOutput, calls=%fused_computation.243 | convolution fusion | flops 2415919104 | bytes 8650752 | tf_op jit(solution)/shard_map/dot_general | solution.py:253
  259.6 6.1 %fusion.61 = (f32[1024]{0:T(1024)S(1)}, f32[1024,768]{0,1:T(8,128)S(1)}) fusion(f32[1024,768]{0,1:T(8,128)} %fusion.62, bf16[1024,1536]{1,0:T(8,128)(2,1)S(1)} %get-tuple-element.213, bf16[1536,768]{1,0:T(8,128)(2,1)} %bitcast.30, f32[768]{0:T(1024)S(1)} %copy-done.33, f32[768]{0:T(1024)S(1)} %copy-done.28, f32[768]{0:T(1024)S(1)} %copy-done.27, ...), kind=kOutput, calls=%fused_computation.242 | convolution fusion | flops 2422209536 | bytes 14963712 | tf_op jit(solution)/shard_map/dot_general | solution.py:253
  272.9 7.7 %convert_reduce_fusion.2 = (bf16[1536]{0:T(1024)(128)(2,1)S(1)}, bf16[1024,1536]{1,0:T(8,128)(2,1)}) fusion(f32[1024,1536]{1,0:T(8,128)S(1)} %get-tuple-element.214, f32[1536]{0:T(1024)S(1)} %copy-done.31, bf16[1024,768]{0,1:T(8,128)(2,1)S(1)} %get-tuple-element.158, bf16[1536,768]{1,0:T(8,128)(2,1)} %bitcast.30), kind=kOutput, calls=%fused_computation.17 | convolution fusion | flops 2436364800 | bytes 13378560 | tf_op jit(solution)/shard_map/dot_general | solution.py:263
  280.6 6.3 %convert_reduce_fusion.1 = (bf16[1536]{0:T(1024)(128)(2,1)S(1)}, bf16[1024,1536]{1,0:T(8,128)(2,1)S(1)}) fusion(f32[1024,1536]{1,0:T(8,128)S(1)} %get-tuple-element.212, f32[1536]{0:T(1024)S(1)} %add.479, bf16[1024,768]{0,1:T(8,128)(2,1)S(1)} %get-tuple-element.158, bf16[1536,768]{1,0:T(8,128)(2,1)} %collective-permute-done.27), kind=kOutput, calls=%fused_computation.16 | convolution fusion | flops 2436364800 | bytes 13378560 | tf_op jit(solution)/shard_map/dot_general | solution.py:263
  292.4 5.7 multiply_reduce_fusion
  316.5 70.7 %attention_backward.1 = bf16[2048,1152]{1,0:T(8,128)(2,1)} custom-call(s32[4]{0:T(128)} %fusion.40.place_ref, s32[8]{0:T(128)} %get-tuple-element.163.start_ref, s32[8]{0:T(128)} %get-tuple-element.164.count_ref, bf16[2048,1152]{1,0:T(8,128)(2,1)} %multiply_convert_fusion.qkv_ref, bf16[2048,384]{1,0:T(8,128)(2,1)} %get-tuple-element.19.ctx_ref, ...), custom_call_target="tpu_custom_call" | custom-call | flops 60000002048 | bytes 15000000 | tf_op jit(solution)/shard_map/attention_backward/pallas_call | solution.py:192
  390.6 7.5 %convolution_convert_fusion.4 = bf16[768,1152]{1,0:T(8,128)(2,1)S(1)} fusion(bf16[2048,1152]{1,0:T(8,128)(2,1)} %attention_backward.1, bf16[512,768]{0,1:T(8,128)(2,1)} %copy-done.37, bf16[512,768]{0,1:T(8,128)(2,1)} %collective-permute-done.1, bf16[512,768]{0,1:T(8,128)(2,1)} %collective-permute-done, bf16[512,768]{0,1:T(8,128)(2,1)} %bitcast), kind=kOutput, calls=%fused_computation.33 | convolution fusion | flops 3637346304 | bytes 9633792 | tf_op jit(solution)/shard_map/dot_general | solution.py:257
  403.0 5.7 convolution_convert_fusion.2
  410.1 14.5 %collective-permute-done.33 = bf16[4,97,1152]{2,0,1:T(4,128)(2,1)S(1)} collective-permute-done((bf16[4,97,1152]{2,0,1:T(4,128)(2,1)S(1)}, bf16[4,97,1152]{2,0,1:T(4,128)(2,1)S(1)}, u32[]{:S(2)}, u32[]{:S(2)}) %collective-permute-start.33) | collective-permute-done | bytes 893984 | tf_op jit(solution)/shard_map/ppermute | solution.py:298
  426.5 8.1 %collective-permute-start.35 = (bf16[97,1152]{1,0:T(8,128)(2,1)}, bf16[97,1152]{1,0:T(8,128)(2,1)}, u32[]{:S(2)}, u32[]{:S(2)}) collective-permute-start(bf16[97,1152]{1,0:T(8,128)(2,1)} %get-tuple-element.188), channel_id=1, source_target_pairs={{0,16},{8,24},{16,0},{24,8},{1,17},{9,25},{17,1},{25,9},{2,18},{10... | collective-permute-start | bytes 670472 | tf_op jit(solution)/shard_map/ppermute | solution.py:298
  441.1 9.4 %collective-permute-done.35 = bf16[97,1152]{1,0:T(8,128)(2,1)} collective-permute-done((bf16[97,1152]{1,0:T(8,128)(2,1)}, bf16[97,1152]{1,0:T(8,128)(2,1)}, u32[]{:S(2)}, u32[]{:S(2)}) %collective-permute-start.35) | collective-permute-done | bytes 223520 | tf_op jit(solution)/shard_map/ppermute | solution.py:298
  452.0 6.9 %fusion.64 = f32[2048,768]{0,1:T(8,128)S(1)} fusion(bf16[2048,1152]{1,0:T(8,128)(2,1)} %attention_backward.1, bf16[768,1152]{1,0:T(8,128)(2,1)} %bitcast.183), kind=kOutput, calls=%fused_computation.245 | convolution fusion | flops 3623878656 | bytes 12779520 | tf_op jit(solution)/shard_map/dot_general | solution.py:263
  472.2 5.9 add_convert_fusion
  510.4 5.7 collective-permute-start.50
  518.5 21.1 %collective-permute-done.41 = bf16[4,96,1920]{2,1,0:T(8,128)(2,1)} collective-permute-done((bf16[4,96,1920]{2,1,0:T(8,128)(2,1)}, bf16[4,96,1920]{2,1,0:T(8,128)(2,1)}, u32[]{:S(2)}, u32[]{:S(2)}) %collective-permute-start.41) | collective-permute-done | bytes 1474592 | tf_op jit(solution)/shard_map/ppermute | solution.py:298
  541.5 5.6 collective-permute-start.42
  556.1 13.4 %collective-permute-done.43 = bf16[96,1920]{1,0:T(8,128)(2,1)S(1)} collective-permute-done((bf16[96,1920]{1,0:T(8,128)(2,1)S(1)}, bf16[96,1920]{1,0:T(8,128)(2,1)S(1)}, u32[]{:S(2)}, u32[]{:S(2)}) %collective-permute-start.43) | collective-permute-done | bytes 368672 | tf_op jit(solution)/shard_map/ppermute | solution.py:298
  573.1 7.0 %collective-permute-done.53 = bf16[192,768]{1,0:T(8,128)(2,1)S(1)} collective-permute-done((bf16[192,768]{1,0:T(8,128)(2,1)S(1)}, bf16[192,768]{1,0:T(8,128)(2,1)S(1)}, u32[]{:S(2)}, u32[]{:S(2)}) %collective-permute-start.53) | collective-permute-done | bytes 294944 | tf_op jit(solution)/shard_map/ppermute | solution.py:302
  (407 shorter events, 276.8 us)
Async XLA Ops:
  4.3 38.3 %collective-permute-start.3 = (bf16[97,1152]{1,0:T(8,128)(2,1)}, bf16[97,1152]{1,0:T(8,128)(2,1)}, u32[]{:S(2)}, u32[]{:S(2)}) collective-permute-start(bf16[97,1152]{1,0:T(8,128)(2,1)} %constant_dynamic-update-slice_fusion), channel_id=1, source_target_pairs={{0,8},{8,16},{16,24},{24,0},{1,9},{9,17},{17,25},{25,1},{2,10},{10... | collective-permute-start | bytes 670472 | tf_op jit(solution)/shard_map/ppermute | solution.py:298
  7.4 37.3 %collective-permute-start.4 = (bf16[97,1152]{1,0:T(8,128)(2,1)}, bf16[97,1152]{1,0:T(8,128)(2,1)}, u32[]{:S(2)}, u32[]{:S(2)}) collective-permute-start(bf16[97,1152]{1,0:T(8,128)(2,1)} %constant_dynamic-update-slice_fusion), channel_id=1, source_target_pairs={{0,16},{8,24},{16,0},{24,8},{1,17},{9,25},{17,1},{25,9},{2,18},{10... | collective-permute-start | bytes 670472 | tf_op jit(solution)/shard_map/ppermute | solution.py:298
  9.9 39.1 %collective-permute-start.5 = (bf16[97,1152]{1,0:T(8,128)(2,1)}, bf16[97,1152]{1,0:T(8,128)(2,1)}, u32[]{:S(2)}, u32[]{:S(2)}) collective-permute-start(bf16[97,1152]{1,0:T(8,128)(2,1)} %constant_dynamic-update-slice_fusion), channel_id=1, source_target_pairs={{0,24},{8,0},{16,8},{24,16},{1,25},{9,1},{17,9},{25,17},{2,26},{10... | collective-permute-start | bytes 670472 | tf_op jit(solution)/shard_map/ppermute | solution.py:298
  11.3 40.0 %collective-permute-start.6 = (bf16[97,1152]{1,0:T(8,128)(2,1)}, bf16[97,1152]{1,0:T(8,128)(2,1)}, u32[]{:S(2)}, u32[]{:S(2)}) collective-permute-start(bf16[97,1152]{1,0:T(8,128)(2,1)} %constant_dynamic-update-slice_fusion), channel_id=1, source_target_pairs={{0,4},{4,0},{1,5},{5,1},{2,6},{6,2},{3,7},{7,3},{8,12},{12,8},{9,1... | collective-permute-start | bytes 670472 | tf_op jit(solution)/shard_map/ppermute | solution.py:298
  18.8 79.3 %collective-permute-start.11 = (bf16[96,1920]{1,0:T(8,128)(2,1)}, bf16[96,1920]{1,0:T(8,128)(2,1)}, u32[]{:S(2)}, u32[]{:S(2)}) collective-permute-start(bf16[96,1920]{1,0:T(8,128)(2,1)} %pad_maximum_fusion.6), channel_id=1, source_target_pairs={{0,8},{8,16},{16,24},{24,0},{1,9},{9,17},{17,25},{25,1},{2,10},{10... | collective-permute-start | bytes 1105928 | tf_op jit(solution)/shard_map/ppermute | solution.py:298
  42.6 56.5 %collective-permute-start.12 = (bf16[96,1920]{1,0:T(8,128)(2,1)}, bf16[96,1920]{1,0:T(8,128)(2,1)S(1)}, u32[]{:S(2)}, u32[]{:S(2)}) collective-permute-start(bf16[96,1920]{1,0:T(8,128)(2,1)} %pad_maximum_fusion.6), channel_id=1, source_target_pairs={{0,16},{8,24},{16,0},{24,8},{1,17},{9,25},{17,1},{25,9},{2,18},{10... | collective-permute-start | bytes 1105928 | tf_op jit(solution)/shard_map/ppermute | solution.py:298
  44.6 55.1 %collective-permute-start.13 = (bf16[96,1920]{1,0:T(8,128)(2,1)}, bf16[96,1920]{1,0:T(8,128)(2,1)S(1)}, u32[]{:S(2)}, u32[]{:S(2)}) collective-permute-start(bf16[96,1920]{1,0:T(8,128)(2,1)} %pad_maximum_fusion.6), channel_id=1, source_target_pairs={{0,24},{8,0},{16,8},{24,16},{1,25},{9,1},{17,9},{25,17},{2,26},{10... | collective-permute-start | bytes 1105928 | tf_op jit(solution)/shard_map/ppermute | solution.py:298
  51.3 36.2 %collective-permute-start.20 = (bf16[192,768]{1,0:T(8,128)(2,1)S(1)}, bf16[192,768]{1,0:T(8,128)(2,1)S(1)}, u32[]{:S(2)}, u32[]{:S(2)}) collective-permute-start(bf16[192,768]{1,0:T(8,128)(2,1)S(1)} %get-tuple-element.162), channel_id=1, source_target_pairs={{0,16},{8,24},{16,0},{24,8},{1,17},{9,25},{17,1},{25,9},{2,18},{10... | collective-permute-start | bytes 884744 | tf_op jit(solution)/shard_map/ppermute | solution.py:298
  95.8 47.2 %collective-permute-start = (bf16[512,768]{0,1:T(8,128)(2,1)}, bf16[512,768]{0,1:T(8,128)(2,1)}, u32[]{:S(2)}, u32[]{:S(2)}) collective-permute-start(bf16[512,768]{0,1:T(8,128)(2,1)} %bitcast.1), channel_id=1, source_target_pairs={{0,2},{2,0},{1,3},{3,1},{4,6},{6,4},{5,7},{7,5},{8,10},{10,8},{9,1... | collective-permute-start | bytes 2359304 | tf_op jit(solution)/shard_map/ppermute | solution.py:302
  98.1 53.9 %collective-permute-start.1 = (bf16[512,768]{0,1:T(8,128)(2,1)}, bf16[512,768]{0,1:T(8,128)(2,1)}, u32[]{:S(2)}, u32[]{:S(2)}) collective-permute-start(bf16[512,768]{0,1:T(8,128)(2,1)} %bitcast), channel_id=1, source_target_pairs={{0,1},{1,0},{2,3},{3,2},{4,5},{5,4},{6,7},{7,6},{8,9},{9,8},{10,11... | collective-permute-start | bytes 2359304 | tf_op jit(solution)/shard_map/ppermute | solution.py:302
  99.2 135.2 %collective-permute-start.29 = (bf16[512,768]{0,1:T(8,128)(2,1)}, bf16[512,768]{0,1:T(8,128)(2,1)}, u32[]{:S(2)}, u32[]{:S(2)}) collective-permute-start(bf16[512,768]{0,1:T(8,128)(2,1)} %bitcast.34), channel_id=1, source_target_pairs={{0,2},{2,0},{1,3},{3,1},{4,6},{6,4},{5,7},{7,5},{8,10},{10,8},{9,1... | collective-permute-start | bytes 2359304 | tf_op jit(solution)/shard_map/ppermute | solution.py:302
  115.5 111.1 %collective-permute-start.23 = (bf16[192,768]{1,0:T(8,128)(2,1)S(1)}, bf16[192,768]{1,0:T(8,128)(2,1)}, u32[]{:S(2)}, u32[]{:S(2)}) collective-permute-start(bf16[192,768]{1,0:T(8,128)(2,1)S(1)} %collective-permute-done.19), channel_id=1, source_target_pairs={{0,4},{4,0},{1,5},{5,1},{2,6},{6,2},{3,7},{7,3},{8,12},{12,8},{9,1... | collective-permute-start | bytes 884744 | tf_op jit(solution)/shard_map/ppermute | solution.py:298
  150.3 78.5 %collective-permute-start.24 = (bf16[192,768]{1,0:T(8,128)(2,1)S(1)}, bf16[192,768]{1,0:T(8,128)(2,1)}, u32[]{:S(2)}, u32[]{:S(2)}) collective-permute-start(bf16[192,768]{1,0:T(8,128)(2,1)S(1)} %collective-permute-done.20), channel_id=1, source_target_pairs={{0,4},{4,0},{1,5},{5,1},{2,6},{6,2},{3,7},{7,3},{8,12},{12,8},{9,1... | collective-permute-start | bytes 884744 | tf_op jit(solution)/shard_map/ppermute | solution.py:298
  152.0 78.5 %collective-permute-start.25 = (bf16[192,768]{1,0:T(8,128)(2,1)}, bf16[192,768]{1,0:T(8,128)(2,1)}, u32[]{:S(2)}, u32[]{:S(2)}) collective-permute-start(bf16[192,768]{1,0:T(8,128)(2,1)} %copy-done.24), channel_id=1, source_target_pairs={{0,4},{4,0},{1,5},{5,1},{2,6},{6,2},{3,7},{7,3},{8,12},{12,8},{9,1... | collective-permute-start | bytes 884744 | tf_op jit(solution)/shard_map/ppermute | solution.py:298
  152.4 73.2 %collective-permute-start.17 = (bf16[96,1920]{1,0:T(8,128)(2,1)}, bf16[96,1920]{1,0:T(8,128)(2,1)S(1)}, u32[]{:S(2)}, u32[]{:S(2)}) collective-permute-start(bf16[96,1920]{1,0:T(8,128)(2,1)} %copy-done.22), channel_id=1, source_target_pairs={{0,4},{4,0},{1,5},{5,1},{2,6},{6,2},{3,7},{7,3},{8,12},{12,8},{9,1... | collective-permute-start | bytes 1105928 | tf_op jit(solution)/shard_map/ppermute | solution.py:298
  308.8 163.4 %collective-permute-start.48 = (bf16[1536,768]{1,0:T(8,128)(2,1)}, bf16[1536,768]{1,0:T(8,128)(2,1)}, u32[]{:S(2)}, u32[]{:S(2)}) collective-permute-start(bf16[1536,768]{1,0:T(8,128)(2,1)} %convolution_convert_fusion), channel_id=1, source_target_pairs={{0,1},{1,0},{2,3},{3,2},{4,5},{5,4},{6,7},{7,6},{8,9},{9,8},{10,11... | collective-permute-start | bytes 7077896 | tf_op jit(solution)/shard_map/ppermute | solution.py:302
  402.4 32.3 %collective-permute-start.39 = (bf16[768,384]{0,1:T(8,128)(2,1)S(1)}, bf16[768,384]{0,1:T(8,128)(2,1)S(1)}, u32[]{:S(2)}, u32[]{:S(2)}) collective-permute-start(bf16[768,384]{0,1:T(8,128)(2,1)S(1)} %constant_dynamic-slice_fusion), channel_id=1, source_target_pairs={{0,1},{1,0},{2,3},{3,2},{4,5},{5,4},{6,7},{7,6},{8,9},{9,8},{10,11... | collective-permute-start | bytes 1769480 | tf_op jit(solution)/shard_map/ppermute | solution.py:302
  408.7 71.1 %collective-permute-start.40 = (bf16[768,1536]{1,0:T(8,128)(2,1)}, bf16[768,1536]{1,0:T(8,128)(2,1)}, u32[]{:S(2)}, u32[]{:S(2)}) collective-permute-start(bf16[768,1536]{1,0:T(8,128)(2,1)} %convolution_convert_fusion.2), channel_id=1, source_target_pairs={{0,1},{1,0},{2,3},{3,2},{4,5},{5,4},{6,7},{7,6},{8,9},{9,8},{10,11... | collective-permute-start | bytes 7077896 | tf_op jit(solution)/shard_map/ppermute | solution.py:302
  463.1 84.1 %collective-permute-start.31 = (bf16[1024,768]{0,1:T(8,128)(2,1)}, bf16[1024,768]{0,1:T(8,128)(2,1)}, u32[]{:S(2)}, u32[]{:S(2)}) collective-permute-start(bf16[1024,768]{0,1:T(8,128)(2,1)} %slice.289), channel_id=1, source_target_pairs={{0,1},{1,0},{2,3},{3,2},{4,5},{5,4},{6,7},{7,6},{8,9},{9,8},{10,11... | collective-permute-start | bytes 4718600 | tf_op jit(solution)/shard_map/ppermute | solution.py:302
  487.1 52.5 %collective-permute-start.41 = (bf16[4,96,1920]{2,1,0:T(8,128)(2,1)}, bf16[4,96,1920]{2,1,0:T(8,128)(2,1)}, u32[]{:S(2)}, u32[]{:S(2)}) collective-permute-start(bf16[4,96,1920]{2,1,0:T(8,128)(2,1)} %dynamic-slice_bitcast_fusion), channel_id=1, source_target_pairs={{0,4},{4,0},{1,5},{5,1},{2,6},{6,2},{3,7},{7,3},{8,12},{12,8},{9,1... | collective-permute-start | bytes 4423688 | tf_op jit(solution)/shard_map/ppermute | solution.py:298
  510.4 36.7 %collective-permute-start.50 = (bf16[192,768]{1,0:T(8,128)(2,1)S(1)}, bf16[192,768]{1,0:T(8,128)(2,1)S(1)}, u32[]{:S(2)}, u32[]{:S(2)}) collective-permute-start(bf16[192,768]{1,0:T(8,128)(2,1)S(1)} %get-tuple-element.180), channel_id=1, source_target_pairs={{0,8},{8,16},{16,24},{24,0},{1,9},{9,17},{17,25},{25,1},{2,10},{10... | collective-permute-start | bytes 884744 | tf_op jit(solution)/shard_map/ppermute | solution.py:298
  516.0 37.1 %collective-permute-start.51 = (bf16[192,768]{1,0:T(8,128)(2,1)S(1)}, bf16[192,768]{1,0:T(8,128)(2,1)S(1)}, u32[]{:S(2)}, u32[]{:S(2)}) collective-permute-start(bf16[192,768]{1,0:T(8,128)(2,1)S(1)} %get-tuple-element.182), channel_id=1, source_target_pairs={{0,16},{8,24},{16,0},{24,8},{1,17},{9,25},{17,1},{25,9},{2,18},{10... | collective-permute-start | bytes 884744 | tf_op jit(solution)/shard_map/ppermute | solution.py:298
  516.0 39.2 %collective-permute-start.52 = (bf16[192,768]{1,0:T(8,128)(2,1)S(1)}, bf16[192,768]{1,0:T(8,128)(2,1)S(1)}, u32[]{:S(2)}, u32[]{:S(2)}) collective-permute-start(bf16[192,768]{1,0:T(8,128)(2,1)S(1)} %get-tuple-element.181), channel_id=1, source_target_pairs={{0,24},{8,0},{16,8},{24,16},{1,25},{9,1},{17,9},{25,17},{2,26},{10... | collective-permute-start | bytes 884744 | tf_op jit(solution)/shard_map/ppermute | solution.py:298
  553.2 34.2 %collective-permute-start.32 = (bf16[512,768]{0,1:T(8,128)(2,1)S(1)}, bf16[512,768]{0,1:T(8,128)(2,1)S(1)}, u32[]{:S(2)}, u32[]{:S(2)}) collective-permute-start(bf16[512,768]{0,1:T(8,128)(2,1)S(1)} %slice.290), channel_id=1, source_target_pairs={{0,2},{2,0},{1,3},{3,1},{4,6},{6,4},{5,7},{7,5},{8,10},{10,8},{9,1... | collective-permute-start | bytes 2359304 | tf_op jit(solution)/shard_map/ppermute | solution.py:302
  (83 other events, 798.5 us)
